TPU v7x, 512 devices: a 8x2x16 block of a 8x8x16 slice. The times are simulated.
512 devices in a mesh: parts: 2 (over y), brick: 16 (over z), rep: 8 (over x), sub: 2 (over core).
Axes of the slice: x: 8, y: 2, z: 16, core: 2. Of those that a mesh axis runs over, the one named last changes fastest.
The devices are a block of a 8x8x16 slice.
Arguments:
- fine_cells: int32 [5, 524288], P(None, ('parts', 'brick', 'rep', 'sub')), parts along dimension 1, may hold values from 0 to 511, as said below
- fine_exponent: float32 [524288], P(('parts', 'brick', 'rep', 'sub')), parts along dimension 0, may hold values from 0.05 to 0.6
- fine_charge: float32 [524288], P(('parts', 'brick', 'rep', 'sub')), parts along dimension 0, may hold values from -6 to 6
- fine_offset: float32 [3, 524288], P(None, ('parts', 'brick', 'rep', 'sub')), parts along dimension 1, may hold values from 0 to 1
- wide_cells: int32 [5, 65536], P(None, ('parts', 'brick', 'rep', 'sub')), parts along dimension 1, may hold values from 0 to 127, as said below
- wide_exponent: float32 [65536], P(('parts', 'brick', 'rep', 'sub')), parts along dimension 0, may hold values from 0.05 to 0.6
- wide_charge: float32 [65536], P(('parts', 'brick', 'rep', 'sub')), parts along dimension 0, may hold values from -6 to 6
- wide_offset: float32 [3, 65536], P(None, ('parts', 'brick', 'rep', 'sub')), parts along dimension 1, may hold values from 0 to 1
Outputs:
- finest_grid: float32 [256, 512, 512], P(('parts', 'brick'), ('rep', 'sub')), parts along dimension 0
- second_grid: float32 [128, 256, 256], P(('parts', 'brick'), ('rep', 'sub')), parts along dimension 0
- middle_grid: float32 [64, 16384], P('parts', 'brick'), parts along dimension 0
- coarse_grid: float32 [32, 4096], P('parts', 'brick'), parts along dimension 0
- coarsest_grid: float32 [16, 1024], P('parts', 'brick'), parts along dimension 0
There are 2 independent parts, one for each index of `parts`. A program takes and returns all parts, laid end to end along the dimension named above; each array names one. Nothing has to cross between parts.
Inputs may be any that keep to these rules, and one draw needn't show every extreme that they name: `fine_cells`: column n is one fine Gaussian: row 0 its level L (0 or 1), row 1 its radius (1 to 4, equal to 4 on every 16th column), rows 2 to 4 its centre cell on level L's grid. The centre lies in the block of the device that holds column n: along the first dimension within that device's brick block of 128/2^L/16 cells, along the second within its block of 512/2^L/16 cells along rep+sub, anywhere along the third. `wide_cells`: column n is one wide Gaussian: row 0 its level L (2 to 4), row 1 its radius (1 to 4, equal to 4 on every 16th column), rows 2 to 4 its centre cell, anywhere on level L's grid.
All inputs are finite; a program needn't handle non-finite values.
Results may differ from a plain program's by a relative error of at most 0.0038.
Values sent between devices are 32-bit elements; how exact they have to be, the bound alone decides.
A program may use at most 64 MiB of HBM per device.

v0:
```python
import math

import jax
import jax.numpy as jnp
from jax import lax
from jax.sharding import PartitionSpec as P

GRID = 512
ROWS = 128
HALF = 4


def shifted(array, axis, by):
    devices = lax.axis_size(axis)
    pairs = [(i, i + by) for i in range(devices) if 0 <= i + by < devices]
    return lax.ppermute(array, axis, pairs)


def shifted_2(array, axis, by):
    devices = lax.axis_size(axis)
    return lax.ppermute(array, axis, [(i, (i + by) % devices) for i in range(devices)])


def copy_for_each(array, axis):
    devices = lax.axis_size(axis)
    return lax.all_to_all(
        jnp.broadcast_to(array[None], (devices, *array.shape)), axis, 0, 0, tiled=True
    )


def laid_out(tiles, dim):
    shape = list(tiles.shape[1:])
    shape[dim] *= tiles.shape[0]
    return jnp.moveaxis(tiles, 0, dim).reshape(shape)


def gather_directly(array, axis, dim):
    tiles = copy_for_each(array, axis)
    return laid_out(tiles, dim)


def taken_together(array, axis):
    everything = copy_for_each(array, axis)
    return jnp.sum(everything, axis=0)


def packed_total(arrays, axis):
    flat, at, outs = (jnp.concatenate([a.reshape(-1) for a in arrays]), 0, [])
    subtotal = taken_together(flat, axis)
    for a in arrays:
        outs.append(subtotal[at : at + a.size].reshape(a.shape))
        at += a.size
    return tuple(outs)


def one_factor(offsets, radius, exponent, centre_shift):
    inside = jnp.abs(offsets) <= radius[:, None]
    spread = offsets.astype(jnp.float32) - centre_shift[:, None]
    return jnp.where(inside, jnp.exp(-exponent[:, None] * spread * spread), 0.0)


def wrapped(positions, anchor, period):
    return jnp.mod(positions[None, :] - anchor[:, None] + period // 2, period) - period // 2


def collocate(slot_table, exponent, charge, offset, level_index, row_cells, col_cells, period):
    slot_count = slot_table.shape[1]
    plane_cells = row_cells.shape[0] * col_cells.shape[0]
    target = max(8, 262144 // plane_cells)
    block_size = math.gcd(slot_count, 1 << target.bit_length() - 1)
    depth_cells = jnp.arange(period, dtype=jnp.int32)

    def add_block(block_index, running):
        first_slot = block_index * block_size
        part_table = lax.dynamic_slice_in_dim(slot_table, first_slot, block_size, 1)
        part_exponent = lax.dynamic_slice_in_dim(exponent, first_slot, block_size, 0)
        part_charge = lax.dynamic_slice_in_dim(charge, first_slot, block_size, 0)
        part_offset = lax.dynamic_slice_in_dim(offset, first_slot, block_size, 1)
        radius = part_table[1]
        masked = jnp.where(part_table[0] == level_index, part_charge, 0.0)
        row_factor = one_factor(
            row_cells[None, :] - part_table[2][:, None], radius, part_exponent, part_offset[0]
        )
        col_factor = one_factor(
            wrapped(col_cells, part_table[3], period), radius, part_exponent, part_offset[1]
        )
        depth_factor = one_factor(
            wrapped(depth_cells, part_table[4], period), radius, part_exponent, part_offset[2]
        )
        plane_weight = ((masked[:, None] * row_factor)[:, :, None] * col_factor[:, None, :]).astype(
            jnp.bfloat16
        )
        plane_weight = plane_weight.reshape(block_size, plane_cells)
        depth_weight = depth_factor.astype(jnp.bfloat16)
        return running + lax.dot_general(
            plane_weight, depth_weight, (((0,), (0,)), ((), ())), preferred_element_type=jnp.float32
        )

    start_grid = jnp.zeros((plane_cells, period), jnp.float32)
    running = lax.fori_loop(0, slot_count // block_size, add_block, start_grid)
    return running.reshape(row_cells.shape[0], col_cells.shape[0], period)


def add_rims(tile_part, from_below, from_above, axis_dim):
    inner_count = tile_part.shape[axis_dim] - 2 * HALF
    interior = lax.slice_in_dim(tile_part, HALF, HALF + inner_count, axis=axis_dim)
    lower_widths = [(0, 0), (0, 0), (0, 0)]
    lower_widths[axis_dim] = (0, inner_count - HALF)
    upper_widths = [(0, 0), (0, 0), (0, 0)]
    upper_widths[axis_dim] = (inner_count - HALF, 0)
    return interior + jnp.pad(from_below, lower_widths) + jnp.pad(from_above, upper_widths)


def fold_rows(first_tile, second_tile):
    from_below = shifted(
        (first_tile[first_tile.shape[0] - HALF :], second_tile[second_tile.shape[0] - HALF :]),
        "brick",
        1,
    )
    from_above = shifted((first_tile[:HALF], second_tile[:HALF]), "brick", -1)
    return (
        add_rims(first_tile, from_below[0], from_above[0], 0),
        add_rims(second_tile, from_below[1], from_above[1], 0),
    )


def fold_columns(first_tile, second_tile):
    from_below = shifted_2(
        (
            first_tile[:, first_tile.shape[1] - HALF :],
            second_tile[:, second_tile.shape[1] - HALF :],
        ),
        ("rep", "sub"),
        1,
    )
    from_above = shifted_2((first_tile[:, :HALF], second_tile[:, :HALF]), ("rep", "sub"), -1)
    return (
        add_rims(first_tile, from_below[0], from_above[0], 1),
        add_rims(second_tile, from_below[1], from_above[1], 1),
    )


def per_device(
    fine_cells,
    fine_exponent,
    fine_charge,
    fine_offset,
    wide_cells,
    wide_exponent,
    wide_charge,
    wide_offset,
):
    brick_count = lax.axis_size("brick")
    column_count = lax.axis_size(("rep", "sub"))
    brick_index = lax.axis_index("brick")
    column_index = lax.axis_index(("rep", "sub"))
    tiles = []
    for level_index in range(2):
        row_tile = (ROWS >> level_index) // brick_count
        period = GRID >> level_index
        col_tile = period // column_count
        row_cells = brick_index * row_tile - HALF + jnp.arange(row_tile + 2 * HALF, dtype=jnp.int32)
        col_cells = (
            column_index * col_tile - HALF + jnp.arange(col_tile + 2 * HALF, dtype=jnp.int32)
        )
        tiles.append(
            collocate(
                fine_cells,
                fine_exponent,
                fine_charge,
                fine_offset,
                level_index,
                row_cells,
                col_cells,
                period,
            )
        )
    gathered_ids = gather_directly(wide_cells, "brick", 1)
    packed = jnp.concatenate([wide_offset, wide_exponent[None, :], wide_charge[None, :]], 0)
    gathered_values = gather_directly(packed, "brick", 1)
    local_shares = []
    for level_index in range(2, 5):
        rows_here = ROWS >> level_index
        period = GRID >> level_index
        share_width = period * period // brick_count
        first_flat = brick_index * share_width
        first_column = first_flat // period
        column_span = min(period, (share_width + period - 1) // period + 1)
        col_cells = first_column + jnp.arange(column_span, dtype=jnp.int32)
        level_grid = collocate(
            gathered_ids,
            gathered_values[3],
            gathered_values[4],
            gathered_values[0:3],
            level_index,
            jnp.arange(rows_here, dtype=jnp.int32),
            col_cells,
            period,
        )
        level_flat = level_grid.reshape(rows_here, column_span * period)
        local_shares.append(
            lax.dynamic_slice_in_dim(level_flat, first_flat - first_column * period, share_width, 1)
        )
    row_folded = fold_rows(tiles[0], tiles[1])
    folded = fold_columns(row_folded[0], row_folded[1])
    shares = packed_total((local_shares[0], local_shares[1], local_shares[2]), ("rep", "sub"))
    return (folded[0], folded[1], shares[0], shares[1], shares[2])


def solution(mesh):
    return jax.shard_map(
        per_device,
        mesh=mesh,
        in_specs=(
            P(None, ("parts", "brick", "rep", "sub")),
            P(("parts", "brick", "rep", "sub")),
            P(("parts", "brick", "rep", "sub")),
            P(None, ("parts", "brick", "rep", "sub")),
            P(None, ("parts", "brick", "rep", "sub")),
            P(("parts", "brick", "rep", "sub")),
            P(("parts", "brick", "rep", "sub")),
            P(None, ("parts", "brick", "rep", "sub")),
        ),
        out_specs=(
            P(("parts", "brick"), ("rep", "sub"), None),
            P(("parts", "brick"), ("rep", "sub"), None),
            P("parts", "brick"),
            P("parts", "brick"),
            P("parts", "brick"),
        ),
        check_vma=False,
    )
```

profile of v0, /device:TPU:65, one launch (start us, length us, event | category | flops | bytes accessed | tf_op | source)
XLA Modules:
  0.0 167.4 jit_solution(17749195121616843513)
XLA Ops:
  0.6 0.7 pad_maximum_fusion.1
  1.4 0.6 broadcast_in_dim.286
  2.0 44.2 %all-to-all-start.1 = ((f32[16,5,128]{2,1,0:T(8,128)}), f32[16,5,128]{2,1,0:T(8,128)S(1)}, u32[]{:S(2)}, u32[]{:S(2)}) async-start(f32[16,5,128]{2,1,0:T(8,128)} %broadcast_in_dim.286), calls=%async_computation.1 | async-start | bytes 131072 | tf_op jit(solution)/shard_map/all_to_all | solution.py:26
  46.3 9.0 %while.62 = (s32[]{:T(128)}, f32[288,256]{1,0:T(8,128)S(1)}, s32[5,1024]{1,0:T(8,128)}, f32[1024]{0:T(1024)}, f32[1024]{0:T(1024)}, /*index=5*/f32[3,1024]{1,0:T...) while((s32[]{:T(128)}, f32[288,256]{1,0:T(8,128)S(1)}, ...), condition=%wide.region_3.4_spmd.clone, body=%wide.region_2.3_spmd.clone.sunk | while | flops 79138352 | bytes 1394253 | solution.py:100
  46.3 0.7 compare_reduce_fusion.7
  47.0 0.8 dynamic-slice_negate_fusion.7
  47.8 0.9 fusion.201
  48.8 0.9 fusion.200
  49.9 0.8 convolution_add_fusion.7
  50.8 0.7 compare_reduce_fusion.7
  51.5 0.8 dynamic-slice_negate_fusion.7
  52.3 0.9 fusion.201
  53.3 0.9 fusion.200
  54.4 0.8 convolution_add_fusion.7
  55.3 3.1 %collective-permute-start.4 = (f32[4,24,256]{2,1,0:T(8,128)S(1)}, f32[4,24,256]{2,1,0:T(8,128)S(1)}, u32[]{:S(2)}, u32[]{:S(2)}) collective-permute-start(f32[4,24,256]{2,1,0:T(8,128)S(1)} %bitcast.163), channel_id=1, source_target_pairs={{0,16},{16,32},{32,48},{48,64},{64,80},{80,96},{96,112},{112,128},... | collective-permute-start | bytes 294920 | tf_op jit(solution)/shard_map/ppermute | solution.py:16
  58.4 1.3 collective-permute-start.5
  59.9 0.6 broadcast_in_dim.283
  60.5 13.6 %all-to-all-start = ((s32[16,5,128]{2,1,0:T(8,128)}), s32[16,5,128]{2,1,0:T(8,128)S(1)}, u32[]{:S(2)}, u32[]{:S(2)}) async-start(s32[16,5,128]{2,1,0:T(8,128)} %broadcast_in_dim.283), calls=%async_computation | async-start | bytes 131072 | tf_op jit(solution)/shard_map/all_to_all | solution.py:26
  74.2 11.3 %all-to-all-done = s32[16,5,128]{2,1,0:T(8,128)S(1)} async-done(((s32[16,5,128]{2,1,0:T(8,128)}), s32[16,5,128]{2,1,0:T(8,128)S(1)}, u32[]{:S(2)}, u32[]{:S(2)}) %all-to-all-start) | async-done | bytes 40992 | tf_op jit(solution)/shard_map/all_to_all | solution.py:26
  86.0 1.3 fusion.127
  87.8 1.3 fusion.129
  89.4 5.2 %while.63 = (s32[]{:T(128)}, f32[288,128]{1,0:T(8,128)S(1)}, s32[5,2048]{1,0:T(8,128)S(1)}, f32[2048]{0:T(1024)S(1)}, f32[2048]{0:T(1024)S(1)}, /*index=5*/f32[3...) while((s32[]{:T(128)}, f32[288,128]{1,0:T(8,128)S(1)}, ...), condition=%wide.region_5.6_spmd.clone, body=%wide.region_4.5_spmd.clone.sunk | while | flops 39804948 | bytes 1709417 | solution.py:100
  90.1 0.6 convolution_add_fusion.8
  91.4 0.6 convolution_add_fusion.8
  92.7 0.6 convolution_add_fusion.8
  94.0 0.6 convolution_add_fusion.8
  94.7 2.7 %broadcast_in_dim.294 = f32[16,1,37376]{2,1,0:T(1,128)} broadcast(f32[37376]{0:T(1024)S(1)} %pad_maximum_fusion), dimensions={2} | broadcast | bytes 2541568 | tf_op jit(solution)/shard_map/broadcast_in_dim | solution.py:27
  97.4 10.6 %all-to-all-start.2 = ((f32[16,1,37376]{2,1,0:T(1,128)}), f32[16,1,37376]{2,1,0:T(1,128)S(1)}, u32[]{:S(2)}, u32[]{:S(2)}) async-start(f32[16,1,37376]{2,1,0:T(1,128)} %broadcast_in_dim.294), calls=%async_computation.2 | async-start | bytes 4784128 | tf_op jit(solution)/shard_map/all_to_all | solution.py:26
  108.0 26.0 %while.61 = (s32[]{:T(128)}, f32[640,512]{1,0:T(8,128)}, s32[5,1024]{1,0:T(8,128)}, f32[1024]{0:T(1024)}, f32[1024]{0:T(1024)}, /*index=5*/f32[3,1024]{1,0:T(4,1...) while((s32[]{:T(128)}, f32[640,512]{1,0:T(8,128)}, ...), condition=%wide.region_1.2_spmd.clone, body=%wide.region_0.1_spmd.clone.sunk | while | flops 171891520 | bytes 3425517 | solution.py:100
  108.0 0.7 compare_reduce_fusion.6
  108.7 0.8 dynamic-slice_negate_fusion.6
  109.4 0.9 fusion.195
  110.4 0.9 fusion.194
  111.5 1.9 %convolution_add_fusion.6 = f32[640,512]{1,0:T(8,128)} fusion(bf16[256,640]{0,1:T(8,128)(2,1)S(1)} %bitcast.128, f32[640,512]{1,0:T(8,128)} %get-tuple-element.1226, pred[]{:T(512)S(6)} %compare.43, f32[256]{0:T(256)S(1)} %bitcast.177, f32[256]{0:T(256)S(1)} %get-tuple-element.1168, s32[256]{0:T(256)S(1)} %bitcast.148, s32[256]{0:T(256)S(1)} %bitcast.178), kind=kOutput, calls=%fused_computation.9.clone.1 | convolution fusion | flops 171311104 | bytes 2953217 | tf_op jit(solution)/shard_map/while/body/eval_jaxpr/dot_general | solution.py:95
  113.5 0.7 compare_reduce_fusion.6
  114.2 0.8 dynamic-slice_negate_fusion.6
  115.0 0.9 fusion.195
  115.9 0.9 fusion.194
  117.0 3.2 %convolution_add_fusion.6 = f32[640,512]{1,0:T(8,128)} fusion(bf16[256,640]{0,1:T(8,128)(2,1)S(1)} %bitcast.128, f32[640,512]{1,0:T(8,128)} %get-tuple-element.1226, pred[]{:T(512)S(6)} %compare.43, f32[256]{0:T(256)S(1)} %bitcast.177, f32[256]{0:T(256)S(1)} %get-tuple-element.1168, s32[256]{0:T(256)S(1)} %bitcast.148, s32[256]{0:T(256)S(1)} %bitcast.178), kind=kOutput, calls=%fused_computation.9.clone.1 | convolution fusion | flops 171311104 | bytes 2953217 | tf_op jit(solution)/shard_map/while/body/eval_jaxpr/dot_general | solution.py:95
  120.3 0.7 compare_reduce_fusion.6
  121.0 0.8 dynamic-slice_negate_fusion.6
  121.8 0.9 fusion.195
  122.7 0.9 fusion.194
  123.9 3.2 %convolution_add_fusion.6 = f32[640,512]{1,0:T(8,128)} fusion(bf16[256,640]{0,1:T(8,128)(2,1)S(1)} %bitcast.128, f32[640,512]{1,0:T(8,128)} %get-tuple-element.1226, pred[]{:T(512)S(6)} %compare.43, f32[256]{0:T(256)S(1)} %bitcast.177, f32[256]{0:T(256)S(1)} %get-tuple-element.1168, s32[256]{0:T(256)S(1)} %bitcast.148, s32[256]{0:T(256)S(1)} %bitcast.178), kind=kOutput, calls=%fused_computation.9.clone.1 | convolution fusion | flops 171311104 | bytes 2953217 | tf_op jit(solution)/shard_map/while/body/eval_jaxpr/dot_general | solution.py:95
  127.1 0.7 compare_reduce_fusion.6
  127.8 0.8 dynamic-slice_negate_fusion.6
  128.6 0.9 fusion.195
  129.5 0.9 fusion.194
  130.7 3.2 %convolution_add_fusion.6 = f32[640,512]{1,0:T(8,128)} fusion(bf16[256,640]{0,1:T(8,128)(2,1)S(1)} %bitcast.128, f32[640,512]{1,0:T(8,128)} %get-tuple-element.1226, pred[]{:T(512)S(6)} %compare.43, f32[256]{0:T(256)S(1)} %bitcast.177, f32[256]{0:T(256)S(1)} %get-tuple-element.1168, s32[256]{0:T(256)S(1)} %bitcast.148, s32[256]{0:T(256)S(1)} %bitcast.178), kind=kOutput, calls=%fused_computation.9.clone.1 | convolution fusion | flops 171311104 | bytes 2953217 | tf_op jit(solution)/shard_map/while/body/eval_jaxpr/dot_general | solution.py:95
  133.9 1.2 fusion.164
  135.1 2.5 %collective-permute-start = (f32[4,40,512]{2,1,0:T(8,128)S(1)}, f32[4,40,512]{2,1,0:T(8,128)S(1)}, u32[]{:S(2)}, u32[]{:S(2)}) collective-permute-start(f32[4,40,512]{2,1,0:T(8,128)S(1)} %bitcast.143), channel_id=1, source_target_pairs={{0,16},{16,32},{32,48},{48,64},{64,80},{80,96},{96,112},{112,128},... | collective-permute-start | bytes 983048 | tf_op jit(solution)/shard_map/ppermute | solution.py:16
  137.6 1.3 collective-permute-start.1
  139.1 1.9 %collective-permute-start.6 = (f32[4,4,256]{2,1,0:T(4,128)S(1)}, f32[4,4,256]{2,1,0:T(4,128)S(1)}, u32[]{:S(2)}, u32[]{:S(2)}) collective-permute-start(f32[4,4,256]{2,1,0:T(4,128)S(1)} %get-tuple-element.999), channel_id=1, source_target_pairs={{0,1},{1,2},{2,3},{3,4},{4,5},{5,6},{6,7},{7,8},{8,9},{9,10},{10,1... | collective-permute-start | bytes 49160 | tf_op jit(solution)/shard_map/ppermute | solution.py:21
  141.0 3.3 %collective-permute-done = f32[4,40,512]{2,1,0:T(8,128)S(1)} collective-permute-done((f32[4,40,512]{2,1,0:T(8,128)S(1)}, f32[4,40,512]{2,1,0:T(8,128)S(1)}, u32[]{:S(2)}, u32[]{:S(2)}) %collective-permute-start) | collective-permute-done | bytes 327712 | tf_op jit(solution)/shard_map/ppermute | solution.py:16
  144.3 3.9 %collective-permute-done.1 = f32[4,40,512]{2,1,0:T(8,128)S(1)} collective-permute-done((f32[4,40,512]{2,1,0:T(8,128)S(1)}, f32[4,40,512]{2,1,0:T(8,128)S(1)}, u32[]{:S(2)}, u32[]{:S(2)}) %collective-permute-start.1) | collective-permute-done | bytes 327712 | tf_op jit(solution)/shard_map/ppermute | solution.py:16
  148.3 2.7 %collective-permute-start.2 = (f32[8,4,512]{2,1,0:T(4,128)S(1)}, f32[8,4,512]{2,1,0:T(4,128)S(1)}, u32[]{:S(2)}, u32[]{:S(2)}) collective-permute-start(f32[8,4,512]{2,1,0:T(4,128)S(1)} %get-tuple-element.994), channel_id=1, source_target_pairs={{0,1},{1,2},{2,3},{3,4},{4,5},{5,6},{6,7},{7,8},{8,9},{9,10},{10,1... | collective-permute-start | bytes 196616 | tf_op jit(solution)/shard_map/ppermute | solution.py:21
  151.1 8.6 %collective-permute-done.6 = f32[4,4,256]{2,1,0:T(4,128)S(1)} collective-permute-done((f32[4,4,256]{2,1,0:T(4,128)S(1)}, f32[4,4,256]{2,1,0:T(4,128)S(1)}, u32[]{:S(2)}, u32[]{:S(2)}) %collective-permute-start.6) | collective-permute-done | bytes 16416 | tf_op jit(solution)/shard_map/ppermute | solution.py:21
  159.6 2.7 %collective-permute-done.7 = f32[4,4,256]{2,1,0:T(4,128)S(1)} collective-permute-done((f32[4,4,256]{2,1,0:T(4,128)S(1)}, f32[4,4,256]{2,1,0:T(4,128)S(1)}, u32[]{:S(2)}, u32[]{:S(2)}) %collective-permute-start.7) | collective-permute-done | bytes 16416 | tf_op jit(solution)/shard_map/ppermute | solution.py:21
  162.3 0.6 fusion.141
  163.0 0.9 fusion.126
  163.9 1.5 reduce_sum.9
  165.4 0.7 reshape.1235
  166.1 0.6 slice.456
  166.7 0.7 reshape.1236
  (117 shorter events, 5.7 us)
Async XLA Ops:
  2.0 57.9 %all-to-all-start.1 = ((f32[16,5,128]{2,1,0:T(8,128)}), f32[16,5,128]{2,1,0:T(8,128)S(1)}, u32[]{:S(2)}, u32[]{:S(2)}) async-start(f32[16,5,128]{2,1,0:T(8,128)} %broadcast_in_dim.286), calls=%async_computation.1 | async-start | bytes 131072 | tf_op jit(solution)/shard_map/all_to_all | solution.py:26
  46.2 13.6 %copy-start.1 = (s32[5,128]{1,0:T(8,128)S(1)}, s32[5,128]{1,0:T(8,128)}, u32[]{:S(2)}) copy-start(s32[5,128]{1,0:T(8,128)} %param.18) | copy-start | bytes 7684
  55.3 83.7 %collective-permute-start.4 = (f32[4,24,256]{2,1,0:T(8,128)S(1)}, f32[4,24,256]{2,1,0:T(8,128)S(1)}, u32[]{:S(2)}, u32[]{:S(2)}) collective-permute-start(f32[4,24,256]{2,1,0:T(8,128)S(1)} %bitcast.163), channel_id=1, source_target_pairs={{0,16},{16,32},{32,48},{48,64},{64,80},{80,96},{96,112},{112,128},... | collective-permute-start | bytes 294920 | tf_op jit(solution)/shard_map/ppermute | solution.py:16
  58.4 80.6 %collective-permute-start.5 = (f32[4,24,256]{2,1,0:T(8,128)S(1)}, f32[4,24,256]{2,1,0:T(8,128)S(1)}, u32[]{:S(2)}, u32[]{:S(2)}) collective-permute-start(f32[4,24,256]{2,1,0:T(8,128)S(1)} %bitcast.162), channel_id=1, source_target_pairs={{16,0},{32,16},{48,32},{64,48},{80,64},{96,80},{112,96},{128,112},... | collective-permute-start | bytes 294920 | tf_op jit(solution)/shard_map/ppermute | solution.py:16
  60.5 25.0 %all-to-all-start = ((s32[16,5,128]{2,1,0:T(8,128)}), s32[16,5,128]{2,1,0:T(8,128)S(1)}, u32[]{:S(2)}, u32[]{:S(2)}) async-start(s32[16,5,128]{2,1,0:T(8,128)} %broadcast_in_dim.283), calls=%async_computation | async-start | bytes 131072 | tf_op jit(solution)/shard_map/all_to_all | solution.py:26
  97.4 66.5 %all-to-all-start.2 = ((f32[16,1,37376]{2,1,0:T(1,128)}), f32[16,1,37376]{2,1,0:T(1,128)S(1)}, u32[]{:S(2)}, u32[]{:S(2)}) async-start(f32[16,1,37376]{2,1,0:T(1,128)} %broadcast_in_dim.294), calls=%async_computation.2 | async-start | bytes 4784128 | tf_op jit(solution)/shard_map/all_to_all | solution.py:26
  133.9 5.0 %copy-start = (f32[640,512]{1,0:T(8,128)S(1)}, f32[640,512]{1,0:T(8,128)}, u32[]{:S(2)}) copy-start(f32[640,512]{1,0:T(8,128)} %get-tuple-element.815) | copy-start | bytes 3932164
  135.1 9.2 %collective-permute-start = (f32[4,40,512]{2,1,0:T(8,128)S(1)}, f32[4,40,512]{2,1,0:T(8,128)S(1)}, u32[]{:S(2)}, u32[]{:S(2)}) collective-permute-start(f32[4,40,512]{2,1,0:T(8,128)S(1)} %bitcast.143), channel_id=1, source_target_pairs={{0,16},{16,32},{32,48},{48,64},{64,80},{80,96},{96,112},{112,128},... | collective-permute-start | bytes 983048 | tf_op jit(solution)/shard_map/ppermute | solution.py:16
  137.6 10.6 %collective-permute-start.1 = (f32[4,40,512]{2,1,0:T(8,128)S(1)}, f32[4,40,512]{2,1,0:T(8,128)S(1)}, u32[]{:S(2)}, u32[]{:S(2)}) collective-permute-start(f32[4,40,512]{2,1,0:T(8,128)S(1)} %bitcast.142), channel_id=1, source_target_pairs={{16,0},{32,16},{48,32},{64,48},{80,64},{96,80},{112,96},{128,112},... | collective-permute-start | bytes 983048 | tf_op jit(solution)/shard_map/ppermute | solution.py:16
  139.1 20.6 %collective-permute-start.6 = (f32[4,4,256]{2,1,0:T(4,128)S(1)}, f32[4,4,256]{2,1,0:T(4,128)S(1)}, u32[]{:S(2)}, u32[]{:S(2)}) collective-permute-start(f32[4,4,256]{2,1,0:T(4,128)S(1)} %get-tuple-element.999), channel_id=1, source_target_pairs={{0,1},{1,2},{2,3},{3,4},{4,5},{5,6},{6,7},{7,8},{8,9},{9,10},{10,1... | collective-permute-start | bytes 49160 | tf_op jit(solution)/shard_map/ppermute | solution.py:21
  141.0 21.3 %collective-permute-start.7 = (f32[4,4,256]{2,1,0:T(4,128)S(1)}, f32[4,4,256]{2,1,0:T(4,128)S(1)}, u32[]{:S(2)}, u32[]{:S(2)}) collective-permute-start(f32[4,4,256]{2,1,0:T(4,128)S(1)} %get-tuple-element.1000), channel_id=1, source_target_pairs={{0,15},{1,0},{2,1},{3,2},{4,3},{5,4},{6,5},{7,6},{8,7},{9,8},{10,9... | collective-permute-start | bytes 49160 | tf_op jit(solution)/shard_map/ppermute | solution.py:21
  148.3 14.6 %collective-permute-start.2 = (f32[8,4,512]{2,1,0:T(4,128)S(1)}, f32[8,4,512]{2,1,0:T(4,128)S(1)}, u32[]{:S(2)}, u32[]{:S(2)}) collective-permute-start(f32[8,4,512]{2,1,0:T(4,128)S(1)} %get-tuple-element.994), channel_id=1, source_target_pairs={{0,1},{1,2},{2,3},{3,4},{4,5},{5,6},{6,7},{7,8},{8,9},{9,10},{10,1... | collective-permute-start | bytes 196616 | tf_op jit(solution)/shard_map/ppermute | solution.py:21
  151.1 11.9 %collective-permute-start.3 = (f32[8,4,512]{2,1,0:T(4,128)S(1)}, f32[8,4,512]{2,1,0:T(4,128)S(1)}, u32[]{:S(2)}, u32[]{:S(2)}) collective-permute-start(f32[8,4,512]{2,1,0:T(4,128)S(1)} %get-tuple-element.995), channel_id=1, source_target_pairs={{0,15},{1,0},{2,1},{3,2},{4,3},{5,4},{6,5},{7,6},{8,7},{9,8},{10,9... | collective-permute-start | bytes 196616 | tf_op jit(solution)/shard_map/ppermute | solution.py:21
where the time goes:
time: 170 us; the launch traced here: 167 us
  starting transfers between devices  81.3 us (48%)
  waiting for transfers between devices  29.8 us (18%)
  local copies, waits for them, and re-layouts  20.1 us (12%)
  matrix products  18.3 us (11%)
  other arithmetic  16.3 us (10%)
    all_to_all x3, starting transfers between devices, copy_for_each(): lax.all_to_all(jnp.broadcast_to(array[None], (devices, *array.shape)), ax...  68.4 us
    dot_general x12, matrix products, add_block(): lax.dot_general(plane_weight, depth_weight, (((0,), (0,)), ((), ())), pre...  18.3 us
    all_to_all x3, waiting for transfers between devices, copy_for_each(): lax.all_to_all(jnp.broadcast_to(array[None], (devices, *array.shape)), ax...  11.3 us
    ppermute x4, waiting for transfers between devices, shifted_2(): lax.ppermute(array, axis, [(i, (i + by) % devices) for i in range(devices)])  11.3 us
    ppermute x4, starting transfers between devices, shifted(): return lax.ppermute(array, axis, pairs)  8.17 us
    ppermute x4, waiting for transfers between devices, shifted(): return lax.ppermute(array, axis, pairs)  7.2 us
    slice x10, local copies, waits for them, and re-layouts, add_block(): part_table[4]  5.92 us
    slice x11, local copies, waits for them, and re-layouts, add_block(): part_offset[2]  5.66 us
  transfers between devices with their start and end apart: 11, of which 6 were waited for; matrix products, arithmetic and copies ran while one was open for 30% of the time, Pallas kernels for 0%

commit v1 on v0

v1 whole, which is shorter than its diff:
```python
import functools

import jax
import jax.numpy as jnp
from jax import lax
from jax.experimental import pallas as pl
from jax.experimental.pallas import tpu as pltpu
from jax.sharding import PartitionSpec as P

GRID = 512
ROWS = 128
HALF = 4
BLOCK = 256
VALUES = 10
MESH = pl.DeviceIdType.MESH
F32 = jnp.float32
BF16 = jnp.bfloat16


def iota(rows, first=0):
    return lax.broadcasted_iota(jnp.int32, (rows, BLOCK), 0).astype(F32) + float(first)


def band_factor(distance, radius, exponent, shift):
    spread = distance - shift
    return jnp.where(jnp.abs(distance) <= radius, jnp.exp(-exponent * spread * spread), 0.0)


def depth_band(centre, period, radius, exponent, shift):
    start = centre - float(HALF)
    start = jnp.where(start < 0.0, start + period, start)
    tile = jnp.floor(start * 0.0625)
    inner = start - 16.0 * tile + float(HALF)
    following = jnp.where((tile + 1.0) * 16.0 >= period, 0.0, tile + 1.0)
    first = band_factor(iota(16) - inner, radius, exponent, shift).astype(BF16)
    second = band_factor(iota(16, 16) - inner, radius, exponent, shift).astype(BF16)
    return tile, following, first, second


def wide_lanes(row):
    return jnp.broadcast_to(row, (16, BLOCK)).astype(BF16)


def dot_depth(plane, depth):
    return lax.dot_general(plane, depth, (((1,), (1,)), ((), ())), preferred_element_type=F32)


def fine_block(values, brick, column, rows, cols):
    level, radius, c0, c1, c2, exponent, charge, s0, s1, s2 = values
    lower = level < 0.5
    rows_f, cols_f = float(rows), float(cols)
    c0 = c0 - jnp.where(lower, rows_f, rows_f / 2) * brick
    c1 = c1 - jnp.where(lower, cols_f, cols_f / 2) * column
    row_factor = band_factor(iota(rows) - c0, radius, exponent, s0)
    inner = band_factor(iota(cols) - c1, radius, exponent, s1)
    eight = iota(8)
    rim_place = jnp.where(eight < 4.0, eight + jnp.where(lower, cols_f, cols_f / 2), eight - 8.0)
    rim = band_factor(rim_place - c1, radius, exponent, s1)
    first_rows = jnp.where(lower, charge, 0.0) * row_factor
    second_rows = jnp.where(lower, 0.0, charge) * row_factor
    first_cols = jnp.concatenate([inner, rim], 0)
    second_cols = jnp.concatenate([inner[: cols // 2], rim], 0)
    plane = [first_rows[i : i + 1] * first_cols for i in range(rows)]
    plane += [second_rows[i : i + 1] * second_cols for i in range(rows // 2)]
    plane = jnp.concatenate(plane, 0).astype(BF16)
    period = jnp.where(lower, float(GRID), float(GRID // 2))
    tile, following, first, second = depth_band(c2, period, radius, exponent, s2)
    tile, following = wide_lanes(tile), wide_lanes(following)
    zero = jnp.zeros((16, BLOCK), BF16)
    depth = [
        jnp.where(tile == BF16(j), first, jnp.where(following == BF16(j), second, zero))
        for j in range(GRID // 16)
    ]
    return dot_depth(plane, jnp.concatenate(depth, 0))


def wide_block(values, brick, bricks):
    level, radius, c0, c1, c2, exponent, charge, s0, s1, s2 = values
    is_two, is_four = level < 2.5, level > 3.5

    def by_level(two, three, four):
        return jnp.where(is_two, two, jnp.where(is_four, four, three))

    period = by_level(128.0, 64.0, 32.0)
    span = GRID // 4 // bricks
    base = by_level(float(span), span / 2.0, span / 4.0) * brick
    distance = iota(8) + base - c1
    distance = jnp.where(distance < -0.5 * period, distance + period, distance)
    distance = jnp.where(distance >= 0.5 * period, distance - period, distance)
    col_factor = band_factor(distance, radius, exponent, s1)
    row_factor = band_factor(iota(32) - c0, radius, exponent, s0)
    two = by_level(charge, 0.0, 0.0) * row_factor
    three = by_level(0.0, charge, 0.0) * row_factor[:16]
    four = by_level(0.0, 0.0, charge) * row_factor[:8]
    plane = [two * col_factor[i : i + 1] for i in range(span)]
    plane += [three * col_factor[i : i + 1] for i in range(span // 2)]
    plane += [four * col_factor[i : i + 1] for i in range(span // 4)]
    plane = jnp.concatenate(plane, 0).astype(BF16)
    tile, following, first, second = depth_band(c2, period, radius, exponent, s2)
    zero = jnp.zeros((16, BLOCK), BF16)
    depth = []
    for j in range(8):
        here = by_level(float(j), float(j % 4), float(j % 2))
        is_first = wide_lanes(tile - here) == BF16(0)
        is_second = wide_lanes(following - here) == BF16(0)
        depth.append(jnp.where(is_first, first, jnp.where(is_second, second, zero)))
    return dot_depth(plane, jnp.concatenate(depth, 0))


def kernel(
    bricks,
    reps,
    fc_ref,
    fe_ref,
    fq_ref,
    fo_ref,
    wc_ref,
    we_ref,
    wq_ref,
    wo_ref,
    finest_ref,
    second_ref,
    middle_ref,
    coarse_ref,
    coarsest_ref,
    fine_pack,
    wide_pack,
    fine_sum,
    wide_sum,
    right_out,
    left_out,
    right_in,
    left_in,
    right_out2,
    left_out2,
    right_in2,
    left_in2,
    share,
    pair_in,
    paired,
    parts_in,
    mine,
    whole,
    fine_send,
    fine_recv,
    wide_send,
    wide_recv,
    rim_send,
    rim_recv,
    pair_send,
    pair_recv,
    part_send,
    part_recv,
    full_send,
    full_recv,
    last_send,
    last_recv,
):
    group = lax.axis_index("parts")
    brick = lax.axis_index("brick")
    rep = lax.axis_index("rep")
    sub = lax.axis_index("sub")
    column = rep * 2 + sub
    other = 1 - sub
    half = bricks // 2
    rows = finest_ref.shape[0]
    cols = finest_ref.shape[1]

    def at_brick(d):
        return (group, lax.rem(brick + d, bricks), rep, sub)

    def at_rep(d):
        return (group, brick, lax.rem(rep + d, reps), sub)

    partner = (group, brick, rep, other)
    right = (group, brick, lax.rem(rep + sub, reps), other)
    left = (group, brick, lax.rem(rep + sub + reps - 1, reps), other)
    outer = (group, brick, lax.rem(rep + 2 * sub + reps - 1, reps), other)

    barrier = pltpu.get_barrier_semaphore()

    def greet(device):
        pl.semaphore_signal(barrier, inc=1, device_id=device, device_id_type=MESH)

    @pl.loop(1, bricks)
    def _(d):
        greet(at_brick(d))

    @pl.loop(1, reps)
    def _(d):
        greet(at_rep(d))

    greet(partner)
    greet(outer)

    def packed(pack, slot, cells, exponent, charge, offset):
        pack[slot, 0:5, :] = cells[...].astype(F32)
        pack[slot, 5:6, :] = exponent[...]
        pack[slot, 6:7, :] = charge[...]
        pack[slot, 7:10, :] = offset[...]

    packed(wide_pack, 0, wc_ref, we_ref, wq_ref, wo_ref)
    packed(fine_pack, 0, fc_ref, fe_ref, fq_ref, fo_ref)

    fine_sum[...] = jnp.zeros_like(fine_sum)
    wide_sum[...] = jnp.zeros_like(wide_sum)
    brick_f = brick.astype(F32)
    column_f = column.astype(F32)
    blocks = fine_pack.shape[2] // BLOCK

    def fine_from(slot):
        @pl.loop(0, blocks)
        def _(i):
            lanes = pl.ds(pl.multiple_of(i * BLOCK, BLOCK), BLOCK)
            values = [fine_pack[slot, v : v + 1, lanes] for v in range(VALUES)]
            fine_sum[...] += fine_block(values, brick_f, column_f, rows, cols)

    def wide_from(first, second):
        values = [
            jnp.concatenate([wide_pack[first, v : v + 1, :], wide_pack[second, v : v + 1, :]], 1)
            for v in range(VALUES)
        ]
        wide_sum[...] += wide_block(values, brick_f, bricks)

    fine_from(0)

    pl.semaphore_wait(barrier, bricks - 1 + reps - 1 + 2)

    def remote(src, dst, send, recv, device):
        return pltpu.make_async_remote_copy(
            src_ref=src,
            dst_ref=dst,
            send_sem=send,
            recv_sem=recv,
            device_id=device,
            device_id_type=MESH,
        )

    def wide_copy(d):
        return remote(
            wide_pack.at[0], wide_pack.at[d], wide_send.at[d], wide_recv.at[d], at_brick(d)
        )

    def fine_copy(slot):
        device = at_brick(1) if slot == 1 else at_brick(bricks - 1)
        return remote(
            fine_pack.at[0], fine_pack.at[slot], fine_send.at[slot], fine_recv.at[slot], device
        )

    wide_copy(half).start()

    @pl.loop(1, half)
    def _(i):
        wide_copy(half - i).start()
        wide_copy(half + i).start()

    fine_copy(1).start()
    fine_copy(2).start()

    for slot in (1, 2):
        fine_copy(slot).wait_recv()
        fine_from(slot)

    span = cols + 8
    for i in range(rows):
        at = i * span + cols
        right_out[4 * i : 4 * i + 4, :] = fine_sum[at : at + 4, :]
        left_out[4 * i : 4 * i + 4, :] = fine_sum[at + 4 : at + 8, :]
    span2 = cols // 2 + 8
    depth2 = second_ref.shape[2]
    for i in range(rows // 2):
        at = rows * span + i * span2 + cols // 2
        right_out2[4 * i : 4 * i + 4, :] = fine_sum[at : at + 4, :depth2]
        left_out2[4 * i : 4 * i + 4, :] = fine_sum[at + 4 : at + 8, :depth2]
    rims = [
        remote(right_out, left_in, rim_send.at[0], rim_recv.at[0], right),
        remote(left_out, right_in, rim_send.at[1], rim_recv.at[1], left),
        remote(right_out2, left_in2, rim_send.at[2], rim_recv.at[2], right),
        remote(left_out2, right_in2, rim_send.at[3], rim_recv.at[3], left),
    ]
    for copy in rims:
        copy.start()

    @pl.loop(1, half)
    def _(i):
        wide_copy(i).wait_recv()
        wide_copy(bricks - i).wait_recv()
        wide_from(i, bricks - i)

    wide_copy(half).wait_recv()
    wide_from(0, half)

    for p in range(16):
        share[p, 0:16, :] = wide_sum[16 * p : 16 * p + 16, :]
    lane = lax.broadcasted_iota(jnp.int32, (8, 128), 1)
    for pair in range(2):
        for h in range(2):
            at = 256 + pair * 32 + 8 * h
            share[2 * pair + h, 16:24, :] = jnp.where(
                lane < 64, wide_sum[at : at + 8, :], wide_sum[at + 16 : at + 24, :]
            )
    share[4, 16:24, :] = jnp.where(lane < 32, wide_sum[320:328, :], wide_sum[328:336, :])
    for p in range(5, 16):
        share[p, 16:24, :] = jnp.zeros((8, 128), F32)

    pair_copy = remote(share.at[pl.ds(other * 8, 8)], pair_in, pair_send, pair_recv, partner)
    pair_copy.start()
    pair_copy.wait_recv()
    paired[...] = share[pl.ds(sub * 8, 8)] + pair_in[...]

    def part_copy(d):
        return remote(
            paired.at[lax.rem(rep + d, reps)],
            parts_in.at[d],
            part_send.at[d],
            part_recv.at[d],
            at_rep(d),
        )

    @pl.loop(1, reps)
    def _(d):
        part_copy(d).start()

    for copy in rims:
        copy.wait_recv()
    for i in range(rows):
        at = i * span
        finest_ref[i, :, :] = fine_sum[at : at + cols, :]
        finest_ref[i, 0:4, :] += left_in[4 * i : 4 * i + 4, :]
        finest_ref[i, cols - 4 : cols, :] += right_in[4 * i : 4 * i + 4, :]
    for i in range(rows // 2):
        at = rows * span + i * span2
        second_ref[i, :, :] = fine_sum[at : at + cols // 2, :depth2]
        second_ref[i, 0:4, :] += left_in2[4 * i : 4 * i + 4, :]
        second_ref[i, cols // 2 - 4 : cols // 2, :] += right_in2[4 * i : 4 * i + 4, :]

    total = paired[rep]
    for d in range(1, reps):
        part_copy(d).wait_recv()
        total = total + parts_in[d]
    mine[...] = total
    slot = sub * 8 + rep
    whole[slot] = total

    def full_copy(d, to):
        return remote(mine, whole.at[to], full_send.at[d], full_recv.at[d], at_rep(d))

    @pl.loop(1, reps)
    def _(d):
        full_copy(d, slot).start()

    @pl.loop(1, reps)
    def _(d):
        full_copy(d, sub * 8 + lax.rem(rep + reps - d, reps)).wait_recv()

    last = remote(
        whole.at[pl.ds(sub * 8, 8)], whole.at[pl.ds(sub * 8, 8)], last_send, last_recv, partner
    )
    last.start()
    last_in = remote(
        whole.at[pl.ds(sub * 8, 8)], whole.at[pl.ds(other * 8, 8)], last_send, last_recv, partner
    )
    last_in.wait_recv()

    for c in range(8):
        for h in range(4):
            t = 4 * c + h
            middle_ref[8 * h : 8 * h + 8, 128 * c : 128 * c + 128] = whole[
                t // 2, 8 * (t % 2) : 8 * (t % 2) + 8, :
            ]
    for pair in range(2):
        for h in range(2):
            coarse_ref[8 * h : 8 * h + 8, 128 * pair : 128 * pair + 128] = whole[
                2 * pair + h, 16:24, :
            ]
    coarsest_ref[...] = whole[4, 16:24, :64]

    @pl.loop(1, bricks)
    def _(d):
        wide_copy(d).wait_send()

    for slot in (1, 2):
        fine_copy(slot).wait_send()
    for copy in rims:
        copy.wait_send()
    pair_copy.wait_send()

    @pl.loop(1, reps)
    def _(d):
        part_copy(d).wait_send()
        full_copy(d, sub * 8 + rep).wait_send()

    last.wait_send()


def per_device(bricks, reps, fc, fe, fq, fo, wc, we, wq, wo):
    columns = reps * 2
    rows, cols = ROWS // bricks, GRID // columns
    fine, wide = fe.shape[0], we.shape[0]
    share = (GRID // 4) ** 2 // bricks
    vmem = pl.BlockSpec(memory_space=pltpu.VMEM)
    dma = pltpu.SemaphoreType.DMA
    tall = rows * (cols + 8) + rows // 2 * (cols // 2 + 8)
    rim, rim2 = (rows * 4, GRID), (rows * 2, GRID // 2)
    return pl.pallas_call(
        functools.partial(kernel, bricks, reps),
        out_shape=(
            jax.ShapeDtypeStruct((rows, cols, GRID), F32),
            jax.ShapeDtypeStruct((rows // 2, cols // 2, GRID // 2), F32),
            jax.ShapeDtypeStruct((ROWS // 4, share), F32),
            jax.ShapeDtypeStruct((ROWS // 8, share // 4), F32),
            jax.ShapeDtypeStruct((ROWS // 16, share // 16), F32),
        ),
        in_specs=[vmem] * 8,
        out_specs=(vmem,) * 5,
        scratch_shapes=[
            pltpu.VMEM((3, VALUES, fine), F32),
            pltpu.VMEM((bricks, VALUES, wide), F32),
            pltpu.VMEM((tall, GRID), F32),
            pltpu.VMEM((336, 128), F32),
            *[pltpu.VMEM(rim, F32) for _ in range(4)],
            *[pltpu.VMEM(rim2, F32) for _ in range(4)],
            pltpu.VMEM((16, 24, 128), F32),
            pltpu.VMEM((8, 24, 128), F32),
            pltpu.VMEM((8, 24, 128), F32),
            pltpu.VMEM((8, 24, 128), F32),
            pltpu.VMEM((24, 128), F32),
            pltpu.VMEM((16, 24, 128), F32),
            dma((3,)),
            dma((3,)),
            dma((bricks,)),
            dma((bricks,)),
            dma((4,)),
            dma((4,)),
            dma,
            dma,
            dma((reps,)),
            dma((reps,)),
            dma((reps,)),
            dma((reps,)),
            dma,
            dma,
        ],
        compiler_params=pltpu.CompilerParams(collective_id=0, has_side_effects=True),
    )(
        fc,
        fe.reshape(1, fine),
        fq.reshape(1, fine),
        fo,
        wc,
        we.reshape(1, wide),
        wq.reshape(1, wide),
        wo,
    )


def solution(mesh):
    everyone = ("parts", "brick", "rep", "sub")
    return jax.shard_map(
        functools.partial(per_device, mesh.shape["brick"], mesh.shape["rep"]),
        mesh=mesh,
        in_specs=(
            P(None, everyone),
            P(everyone),
            P(everyone),
            P(None, everyone),
            P(None, everyone),
            P(everyone),
            P(everyone),
            P(None, everyone),
        ),
        out_specs=(
            P(("parts", "brick"), ("rep", "sub"), None),
            P(("parts", "brick"), ("rep", "sub"), None),
            P("parts", "brick"),
            P("parts", "brick"),
            P("parts", "brick"),
        ),
        check_vma=False,
    )
```

time: 170 us -> 78.9 us (0.46); the launches traced: 167 us -> 78.6 us
  starting transfers between devices: 81.3 us -> 0 us
  Pallas kernels: 0 us -> 73.1 us
  waiting for transfers between devices: 29.8 us -> 0 us
  matrix products: 18.3 us -> 0 us
  other arithmetic: 16.3 us -> 0 us
  local copies, waits for them, and re-layouts: 20.1 us -> 4.81 us
    pallas_call x0 -> x1, Pallas kernels: none -> 73.1 us  [per_device(): pl.pallas_call(functools.partial(kernel, bricks, reps), out_shape=(jax.Sh...]
    all_to_all x3 -> x0, starting transfers between devices: 68.4 us -> none  [copy_for_each(): lax.all_to_all(jnp.broadcast_to(array[None], (devices, *array.shape)), ax...]
    ppermute x8 -> x0, waiting for transfers between devices: 18.5 us -> none  [the longest x4 11.3 us: shifted_2(): lax.ppermute(array, axis, [(i, (i + by) % devices) for i in range(devices)])]
    dot_general x12 -> x0, matrix products: 18.3 us -> none  [add_block(): lax.dot_general(plane_weight, depth_weight, (((0,), (0,)), ((), ())), pre...]
    slice x31 -> x0, local copies, waits for them, and re-layouts: 13.5 us -> none  [the longest x10 5.92 us: add_block(): part_table[4]]
    ppermute x8 -> x0, starting transfers between devices: 12.9 us -> none  [the longest x4 8.17 us: shifted(): return lax.ppermute(array, axis, pairs)]
    all_to_all x3 -> x0, waiting for transfers between devices: 11.3 us -> none  [copy_for_each(): lax.all_to_all(jnp.broadcast_to(array[None], (devices, *array.shape)), ax...]
    neg x11 -> x0, other arithmetic: 5 us -> none  [one_factor(): return jnp.where(inside, jnp.exp(-exponent[:, None] * spread * spread), 0.0)]
  transfers between devices with their start and end apart: 11 -> 0, of which waited for: 6 -> 0; matrix products, arithmetic and copies ran while one was open for 30% -> 0% of each run, Pallas kernels for 0% -> 0%
where the time goes in v1:
time: 78.9 us; the launch traced here: 78.6 us
  Pallas kernels  73.1 us (93%)
  local copies, waits for them, and re-layouts  4.81 us (6%)
    pallas_call x1, Pallas kernels, per_device(): pl.pallas_call(functools.partial(kernel, bricks, reps), out_shape=(jax.Sh...  73.1 us
    unnamed x13, local copies, waits for them, and re-layouts  4.81 us

profile of v1, /device:TPU:65, one launch (start us, length us, event | category | flops | bytes accessed | tf_op | source)
XLA Modules:
  0.0 78.6 jit_solution(8433704663026768411)
XLA Ops:
  0.6 73.1 %shard_map.119 = (f32[8,32,512]{2,1,0:T(8,128)}, f32[4,16,256]{2,1,0:T(8,128)}, f32[32,1024]{1,0:T(8,128)}, f32[16,256]{1,0:T(8,128)}, f32[8,64]{1,0:T(8,128)}) custom-call(s32[5,1024]{1,0:T(8,128)} %fc_ref.1, f32[1,1024]{1,0:T(1,128)} %bitcast.4, f32[1,1024]{1,0:T(1,128)} %bitcast.5, f32[3,1024]{1,0:T(4,128)} %fo_ref.1, s32[5,128]{1,0:T(8,128)} %wc_ref.1, ...), custom_call_target="tpu_custom_call" | custom-call | tf_op jit(solution)/shard_map/pallas_call | solution.py:405
  73.8 0.0 copy-start.1
  73.8 1.9 %copy.18 = f32[8,32,512]{2,1,0:T(8,128)} copy(f32[8,32,512]{2,1,0:T(8,128)} %get-tuple-element.10) | data formatting | bytes 1048576
  75.7 0.0 copy-done.1
  75.7 0.0 copy-start
  75.7 0.6 copy.19
  76.3 0.3 copy-done
  76.6 0.0 copy-start.2
  76.6 0.7 copy.20
  77.3 0.1 copy-done.2
  77.3 0.0 copy-start.3
  77.3 0.6 copy.21
  77.9 0.1 copy-done.3
  78.0 0.6 copy.22
Async XLA Ops:
  73.8 1.9 %copy-start.1 = (f32[4,16,256]{2,1,0:T(8,128)S(1)}, f32[4,16,256]{2,1,0:T(8,128)}, u32[]{:S(2)}) copy-start(f32[4,16,256]{2,1,0:T(8,128)} %get-tuple-element.11) | copy-start | bytes 196612
  75.7 0.9 %copy-start = (f32[32,1024]{1,0:T(8,128)S(1)}, f32[32,1024]{1,0:T(8,128)}, u32[]{:S(2)}) copy-start(f32[32,1024]{1,0:T(8,128)} %get-tuple-element.12) | copy-start | bytes 393220
  76.6 0.7 copy-start.2
  77.3 0.7 copy-start.3
